TPU v7x, 32 devices: a whole 2x2x4 slice. The times are simulated.
32 devices in a mesh: tm: 4 (over z), sx: 4 (over y, x), sy: 2 (over core).
Axes of the slice: x: 2, y: 2, z: 4, core: 2. Of those that a mesh axis runs over, the one named last changes fastest.
Arguments:
- thickness_guess: float32 [4, 1024, 256], P('tm', 'sx', 'sy'), may hold values from 0.5 to 1.5
- thickness_start: float32 [1024, 256], P('sx', 'sy'), may hold values from 0.5 to 1.5
- bed: float32 [1024, 256], P('sx', 'sy'), may hold values from -1.8 to 1.8
- rate_factor: float32 [1024, 256], P('sx', 'sy'), may hold values from 0.05 to 0.5
- mass_balance: float32 [4, 1024, 256], P('tm', 'sx', 'sy'), may hold values from -1.2 to 1.2
- cell_flags: int32 [1024, 256], P('sx', 'sy'), may hold values from 0 to 2, as said below
Outputs:
- thickness: float32 [4, 1024, 256], P('tm', 'sx', 'sy')
Inputs may be any that keep to these rules, and one draw needn't show every extreme that they name: `cell_flags`: 0 marks ice-free cells outside the glacier, 1 ice on bedrock, 2 ice on soft sediment.
All inputs are finite; a program needn't handle non-finite values.
Results may differ from a plain program's by a relative error of at most 0.00015.
Values sent between devices are 32-bit elements; how exact they have to be, the bound alone decides.
No kernel may reach another device: no remote copies, remote signals or barrier semaphores. Data moves between devices by JAX's collectives and lax.ppermute only.
A program may use at most 64 MiB of HBM per device.

v0:
```python
import functools
import math

import jax
import jax.numpy as jnp
from jax import lax
from jax.experimental import pallas as pl
from jax.experimental.pallas import tpu as pltpu
from jax.sharding import PartitionSpec as P


NEWTON = 2
SWEEPS = 8
HALO = NEWTON * SWEEPS
SUB = 8

circulant_weight = 0.25
time_step = 1.0


vmem = pl.BlockSpec(memory_space=pltpu.VMEM)
hbm = pl.BlockSpec(memory_space=pltpu.HBM)
params = pltpu.CompilerParams(vmem_limit_bytes=16 * 1024 * 1024)

fetching = pltpu.CompilerParams(vmem_limit_bytes=56125000)


def struct(*shape):
    return jax.ShapeDtypeStruct(shape, jnp.float32)


def aligned(index):
    return pl.multiple_of(index, SUB)


def strip_of(levels, tm):
    return jnp.where(lax.rem(lax.axis_index("sx"), 2) == 0, tm, levels - 1 - tm)


def level_of(levels, shift):
    return lax.rem(lax.axis_index("tm") + levels - shift, levels)


def pick(array, index):
    return jnp.take_along_axis(array, index, axis=1, mode="promise_in_bounds")


def pack_kernel(levels, strip, *refs):
    guess, balance, start, bed, rate, flags = refs[:6]
    strips = refs[6 : 6 + levels]
    fixed, ice, kind, sems = refs[6 + levels :]
    me = lax.axis_index("tm")

    def rows_of(tm):
        return pl.ds(aligned(strip_of(levels, tm) * strip), strip)

    copies = []
    for shift in range(levels):
        here = rows_of(lax.rem(me + shift, levels))
        copies += [(guess.at[0, here], strips[shift].at[0]), (balance.at[0, here], strips[shift].at[1])]
    here = rows_of(me)
    copies += [
        (start.at[here], fixed.at[0]),
        (bed.at[here], fixed.at[1]),
        (rate.at[here], ice),
        (flags.at[here], kind),
    ]
    copies = [pltpu.make_async_copy(a, b, sems.at[i]) for i, (a, b) in enumerate(copies)]
    for copy in copies:
        copy.start()
    for copy in copies:
        copy.wait()
    boost = jnp.where(kind[...] == 2, 2.0, 1.0)
    fixed[2] = jnp.where(kind[...] != 0, boost * ice[...], 0.0)
    cols = fixed.shape[2]
    lane = lax.broadcasted_iota(jnp.int32, (SUB, cols), 1)
    parting = jnp.where(lane < cols // 2, 2 * lane, 2 * lane - (cols - 1))
    for ref in (*strips, fixed):
        for index in range(ref.shape[0]):
            for row in range(0, strip, SUB):
                ref[index, row : row + SUB] = pick(ref[index, row : row + SUB], parting)


def lay(levels, out, rows, strips, fixed, source):
    for shift in range(levels):
        level = level_of(levels, shift)
        out[level, rows] = strips[shift][0, source]
        out[levels + level, rows] = strips[shift][1, source]
    out[2 * levels :, rows] = fixed[:, source]


def give_kernel(*refs):
    out, place = refs[-1], 0
    keep = out.shape[1]
    for ref in refs[:-1]:
        count, strip, _ = ref.shape
        first = aligned((1 - lax.axis_index("sy")) * (strip - keep))
        out[place : place + count] = ref[:, pl.ds(first, keep)]
        place += count


def lay_taken(levels, out, index, early, late, source):
    for shift in range(levels):
        level = level_of(levels, shift)
        ref, place = (early, 2 * shift) if shift < levels - 1 else (late, 0)
        out[(level, *index)] = ref[place, source]
        out[(levels + level, *index)] = ref[place + 1, source]
    out[(slice(2 * levels, None), *index)] = early[2 * levels - 2 :, source]


def edge_kernel(levels, *refs):
    strips, fixed, early, late, out = refs[:levels], *refs[levels:]
    strip, keep = fixed.shape[1], late.shape[1]
    part = lax.axis_index("sy")
    lay_taken(levels, out, (0,), early, late, pl.ds(aligned(part * (keep - HALO)), HALO))
    source = pl.ds(aligned(part * (strip - HALO)), HALO)
    lay(levels, out.at[:, 1], slice(0, HALO), strips, fixed, source)


def rim_kernel(levels, counts, *refs):
    strips = refs[:levels]
    fixed = refs[levels]
    lows, highs = refs[levels + 1 : levels + 1 + len(counts)], refs[levels + 1 + len(counts) :]
    strip = fixed.shape[1]
    for count, low, high in zip(counts, lows, highs):
        lay(levels, low, slice(0, count), strips, fixed, slice(0, count))
        lay(levels, high, slice(0, count), strips, fixed, slice(strip - count, strip))


def join_kernel(levels, counts, *refs):
    strips = refs[:levels]
    fixed = refs[levels]
    aboves, belows = refs[levels + 1 : levels + 1 + len(counts)], refs[levels + 1 + len(counts) : -1]
    out = refs[-1]
    strip = fixed.shape[1]
    lay(levels, out, slice(HALO, HALO + strip), strips, fixed, slice(0, strip))
    done = 0
    for count, above, below in zip(counts, aboves, belows):
        out[:, HALO - done - count : HALO - done] = above[...]
        out[:, HALO + strip + done : HALO + strip + done + count] = below[...]
        done += count


def mode_fields(levels):
    fields, count = [], 0
    for mode in range(levels // 2 + 1):
        if 2 * mode % levels == 0:
            fields.append((mode, count, None))
            count += 1
        else:
            fields.append((mode, count, count + 1))
            count += 2
    return fields, count


def wave(levels, product):
    product %= levels
    quarter = 4 * product
    if quarter % levels == 0:
        return ((1.0, 0.0), (0.0, 1.0), (-1.0, 0.0), (0.0, -1.0))[quarter // levels]
    angle = 2.0 * math.pi * product / levels
    return math.cos(angle), math.sin(angle)


def combine(terms):
    total = None
    for coeff, value in terms:
        if coeff == 0.0:
            continue
        if total is None:
            total = value if coeff == 1.0 else coeff * value
        elif coeff == 1.0:
            total = total + value
        elif coeff == -1.0:
            total = total - value
        else:
            total = total + coeff * value
    return total


def scratches(levels, depth, cols, high):
    _, field_count = mode_fields(levels)
    shapes = [(count, depth, 2, SUB, cols) for count in (levels, levels, 3, levels, 5, *(field_count,) * 4)]
    shapes.append((4, levels, depth, SUB, cols))
    shapes.append((levels, 2, high, cols))
    return [pltpu.VMEM(shape, jnp.float32) for shape in shapes]


def newton_steps(levels, load, spaces):
    height, balance, fixed, diff, weight, inverse, source, value, side, sides, plain = spaces
    depth, _, _, cols = height.shape[1:]
    across = 2 * cols
    lane = lax.broadcasted_iota(jnp.int32, (SUB, cols), 1)
    low = lane < cols // 2
    column = lax.axis_index("sy") * cols
    first = 2 * lane == lax.rem(across - column, across)
    last = 2 * lane + 1 == across - 1 - column
    fields, field_count = mode_fields(levels)
    root = circulant_weight ** (1.0 / levels)

    def half_turn(array):
        return pltpu.roll(array, cols // 2, axis=1)

    def before(odd):
        return pltpu.roll(odd, 1, axis=1)

    def after(even):
        return pltpu.roll(even, cols - 1, axis=1)

    def from_above(array):
        return pltpu.roll(array, 1, axis=0)

    def from_below(array):
        return pltpu.roll(array, SUB - 1, axis=0)

    def rows_around(read):
        blocks = [read(q) for q in range(depth)]
        return [from_above(blocks[-1])] + blocks + [from_below(blocks[0])]

    places = [(height, level, level) for level in range(levels)]
    places += [(balance, level, levels + level) for level in range(levels)]
    places += [(fixed, index, 2 * levels + index) for index in range(3)]
    for ref, index, field in places:
        for q in range(depth):
            left, right = (load(field, half, q) for half in range(2))
            ref[index, q, 0] = jnp.where(low, left, half_turn(right))
            ref[index, q, 1] = jnp.where(low, half_turn(left), right)

    def newton(step, carry):
        for q in range(depth):
            totals = [None] * 4
            for level in range(levels):
                thick = [height[level, q, r] for r in range(2)]
                d = [fixed[2, q, r] * thick[r] * thick[r] * jnp.abs(thick[r]) for r in range(2)]
                s = [thick[r] + fixed[1, q, r] for r in range(2)]
                for r in range(2):
                    diff[level, q, r] = d[r]
                d_left, d_right = jnp.where(first, 0.0, before(d[1])), jnp.where(last, 0.0, after(d[0]))
                sides[0, level, q] = d_left
                sides[1, level, q] = d_right
                sides[2, level, q] = jnp.where(first, 0.0, before(s[1]))
                sides[3, level, q] = jnp.where(last, 0.0, after(s[0]))
                for i, part in enumerate((d[0], d[1], d_left, d_right)):
                    totals[i] = part if level == 0 else totals[i] + part
            even, odd, left, right = (total * (0.5 / levels) for total in totals)
            weight[0, q, 0], weight[0, q, 1] = even, odd
            weight[4, q, 0], weight[4, q, 1] = left, right
        for r in range(2):
            halves = rows_around(lambda q: weight[0, q, r])
            downs = [halves[q] + halves[q + 1] for q in range(depth + 1)]
            others = [weight[0, q, 1 - r] for q in range(depth)]
            for q in range(depth):
                here, up, down = halves[q + 1], downs[q], downs[q + 1]
                inner, outer = here + others[q], here + weight[4, q, r]
                weight[1, q, r] = up
                weight[2, q, r] = down
                if r == 0:
                    weight[3, q, 0] = inner
                weight[4, q, r] = jnp.where(last if r else first, 0.0, outer)
                total = (up + down) + (inner + outer)
                inside = jnp.where(fixed[2, q, r] > 0.0, 1.0, 0.0)
                for mode, real, imag in fields:
                    cosine, sine = wave(levels, mode)
                    denom = total + (1.0 - root * cosine) / time_step
                    if imag is None:
                        inverse[real, q, r] = inside / denom
                    else:
                        shift = root * sine / time_step
                        ratio = inside / (denom * denom + shift * shift)
                        inverse[real, q, r] = ratio * denom
                        inverse[imag, q, r] = ratio * -shift
        for level in range(levels):
            ds, ss, inners = [], [], []
            for r in range(2):
                ds.append(rows_around(lambda q: diff[level, q, r]))
                ss.append(rows_around(lambda q: height[level, q, r] + fixed[1, q, r]))
            for q in range(depth):
                inners.append((ds[0][q + 1] + ds[1][q + 1]) * (ss[0][q + 1] - ss[1][q + 1]))
            for r in range(2):
                d, s = ds[r], ss[r]
                downs = [(d[q] + d[q + 1]) * (s[q] - s[q + 1]) for q in range(depth + 1)]
                for q in range(depth):
                    outer = (d[q + 1] + sides[r, level, q]) * (s[q + 1] - sides[2 + r, level, q])
                    across_flux = outer - inners[q] if r else outer + inners[q]
                    prior = height[level - 1, q, r] if level > 0 else fixed[0, q, r]
                    change = (
                        (height[level, q, r] - prior) / time_step
                        + 0.5 * ((downs[q + 1] - downs[q]) + across_flux)
                        - balance[level, q, r]
                    )
                    scaled = change if level == 0 else change * root**level
                    source_part = jnp.where(fixed[2, q, r] > 0.0, scaled, 0.0)
                    diff[level, q, r] = source_part

        def put(f, q, parts):
            value[f, q, 0], value[f, q, 1] = parts
            side[f, q, 0], side[f, q, 1] = before(parts[1]), after(parts[0])

        for q in range(depth):
            scaled = [[diff[level, q, r] for level in range(levels)] for r in range(2)]
            for mode, real, imag in fields:
                waves = [wave(levels, mode * level) for level in range(levels)]
                y_real = [combine([(w[0], v) for w, v in zip(waves, scaled[r])]) for r in range(2)]
                i_real = [inverse[real, q, r] for r in range(2)]
                for r in range(2):
                    source[real, q, r] = y_real[r]
                if imag is None:
                    put(real, q, [i_real[r] * y_real[r] for r in range(2)])
                else:
                    y_imag = [combine([(-w[1], v) for w, v in zip(waves, scaled[r])]) for r in range(2)]
                    i_imag = [inverse[imag, q, r] for r in range(2)]
                    for r in range(2):
                        source[imag, q, r] = y_imag[r]
                    put(real, q, [y_real[r] * i_real[r] - y_imag[r] * i_imag[r] for r in range(2)])
                    put(imag, q, [y_real[r] * i_imag[r] + y_imag[r] * i_real[r] for r in range(2)])

        def sweep(index, carry):
            tops = [[value[f, 0, r] for r in range(2)] for f in range(field_count)]
            befores = [[from_above(value[f, depth - 1, r]) for r in range(2)] for f in range(field_count)]
            heres = tops
            for q in range(depth):
                inner = weight[3, q, 0]
                numer, nexts = [], []
                for f in range(field_count):
                    if q + 1 < depth:
                        nexts.append([value[f, q + 1, r] for r in range(2)])
                    else:
                        nexts.append([from_below(tops[f][r]) for r in range(2)])
                    numer.append([
                        source[f, q, r]
                        + ((weight[1, q, r] * befores[f][r] + weight[2, q, r] * nexts[f][r])
                        + (inner * heres[f][1 - r] + weight[4, q, r] * side[f, q, r]))
                        for r in range(2)
                    ])
                for mode, real, imag in fields:
                    i_real = [inverse[real, q, r] for r in range(2)]
                    if imag is None:
                        put(real, q, [i_real[r] * numer[real][r] for r in range(2)])
                    else:
                        i_imag = [inverse[imag, q, r] for r in range(2)]
                        put(real, q, [numer[real][r] * i_real[r] - numer[imag][r] * i_imag[r] for r in range(2)])
                        put(imag, q, [numer[real][r] * i_imag[r] + numer[imag][r] * i_real[r] for r in range(2)])
                befores, heres = heres, nexts
            return carry

        lax.fori_loop(0, SWEEPS - 1, sweep, 0, unroll=levels <= 8)
        for q in range(depth):
            for r in range(2):
                values = [value[f, q, r] for f in range(field_count)]
                for level in range(levels):
                    scale = 1.0 / (levels * root**level)
                    terms = []
                    for mode, real, imag in fields:
                        cosine, sine = wave(levels, mode * level)
                        if imag is None:
                            terms.append((-scale * cosine, values[real]))
                        else:
                            terms.append((-2.0 * scale * cosine, values[real]))
                            terms.append((2.0 * scale * sine, values[imag]))
                    height[level, q, r] = height[level, q, r] + combine(terms)
        return carry

    lax.fori_loop(0, NEWTON, newton, 0)
    for level in range(levels):
        for q in range(depth):
            even, odd = height[level, q, 0], height[level, q, 1]
            rows = pl.ds(q, SUB, stride=depth)
            plain[level, 0, rows, :] = jnp.where(low, even, half_turn(odd))
            plain[level, 1, rows, :] = jnp.where(low, half_turn(even), odd)
    return plain


def newton_kernel(levels, *refs):
    strips, fixed, early, late, halo = refs[:levels], *refs[levels : levels + 4]
    outs = refs[levels + 4 : 2 * levels + 5]
    window, spaces = refs[2 * levels + 5], refs[2 * levels + 6 :]
    strip, keep = fixed.shape[1], late.shape[1]
    me, part = lax.axis_index("tm"), lax.axis_index("sy")
    depth = (HALO + keep) // SUB
    rows = slice(HALO, HALO + keep)
    window[:, :, :HALO] = halo[...]
    lay_taken(levels, window, (1, rows), early, late, slice(0, keep))
    lay(levels, window.at[:, 0], rows, strips, fixed, pl.ds(aligned(part * (strip - keep)), keep))
    plain = newton_steps(levels, lambda field, half, q: window[field, half, pl.ds(q, SUB, stride=depth), :], spaces)
    first = aligned(HALO + part * (keep - strip // 2))
    for shift in range(levels):
        target = lax.rem(me + shift, levels)
        if shift < levels - 1:
            outs[shift][...] = plain[target, :, pl.ds(first, strip // 2)]
        else:
            outs[shift][...] = plain[target, 0, pl.ds(first, strip // 2)]
            outs[shift + 1][...] = plain[target, 1, pl.ds(first, strip // 2)]


def newton_wide_kernel(levels, strip, *refs):
    blocks, outs, spaces = refs[:2], refs[2 : 2 + levels], refs[2 + levels :]
    me = lax.axis_index("tm")
    depth = blocks[0].shape[1] // SUB
    plain = newton_steps(levels, lambda field, half, q: blocks[half][field, pl.ds(q, SUB, stride=depth), :], spaces)
    for shift in range(levels):
        target = lax.rem(me + shift, levels)
        outs[shift][...] = plain[target, 0, HALO : HALO + strip]


def merge_kernel(own, other, out):
    half = own.shape[0]
    part = lax.axis_index("sy")
    out[pl.ds(aligned(part * half), half)] = own[...]
    out[pl.ds(aligned((1 - part) * half), half)] = other[...]


def trade_kernel(*refs):
    out = refs[-1]
    for index, ref in enumerate(refs[:-1]):
        out[index] = ref[1]


def place_kernel(levels, strip, *refs):
    pieces, others, out = refs[:levels], refs[levels:-1], refs[-1]
    part = lax.axis_index("sy")
    cols = out.shape[2]
    lane = lax.broadcasted_iota(jnp.int32, (SUB, cols), 1)
    mixing = lane // 2 + lane % 2 * (cols // 2)

    def put(first, piece):
        for row in range(0, piece.shape[0], SUB):
            out[0, pl.ds(aligned(first + row), SUB)] = pick(piece[row : row + SUB], mixing)

    for shift in range(levels):
        first = strip_of(levels, level_of(levels, shift)) * strip
        if others and shift < levels - 1:
            half = strip // 2
            put(first + part * half, pieces[shift].at[0])
            put(first + (1 - part) * half, others[0].at[shift])
        else:
            put(first, pieces[shift])


def call(kernel, outs, *operands, scratch=(), spec=vmem, params=params):
    return pl.pallas_call(
        kernel,
        out_shape=outs,
        in_specs=[spec] * len(operands),
        out_specs=[vmem] * len(outs) if isinstance(outs, list) else vmem,
        scratch_shapes=list(scratch),
        compiler_params=params,
    )(*operands)


def body(sizes, thickness_guess, thickness_start, bed, rate_factor, mass_balance, cell_flags):
    levels, tiles, parts = sizes
    assert parts == 2
    rows, cols = thickness_start.shape
    strip = rows // levels
    count = 2 * levels + 3
    keep = strip // 2 + HALO

    def swap(value):
        return lax.ppermute(value, "sy", [(0, 1), (1, 0)])

    def around(value, shift):
        return lax.ppermute(value, "tm", [(i, (i + shift) % levels) for i in range(levels)])

    snake = [
        (tm if tile % 2 == 0 else levels - 1 - tm, tile) for tile in range(tiles) for tm in range(levels)
    ]

    def device(place, part):
        tm, tile = snake[place]
        return (tm * tiles + tile) * parts + part

    def along(value, moves):
        pairs = []
        for place in range(len(snake)):
            for part, other, hops in moves:
                if 0 <= place + hops < len(snake):
                    pairs.append((device(place, part), device(place + hops, other)))
        return lax.ppermute(value, ("tm", "sx", "sy"), pairs)

    packed = call(
        functools.partial(pack_kernel, levels, strip),
        [struct(2, strip, cols)] * levels + [struct(3, strip, cols)],
        thickness_guess, mass_balance, thickness_start, bed, rate_factor, cell_flags,
        scratch=(
            pltpu.VMEM((strip, cols), jnp.float32),
            pltpu.VMEM((strip, cols), jnp.int32),
            pltpu.SemaphoreType.DMA((2 * levels + 4,)),
        ),
        spec=hbm,
        params=fetching,
    )
    strips, fixed = packed[:levels], packed[levels]
    strips = [strips[0]] + [around(strips[shift], shift) for shift in range(1, levels)]

    if strip % (2 * SUB) == 0 and keep <= strip:
        def give(*arrays):
            total = sum(array.shape[0] for array in arrays)
            return swap(call(give_kernel, struct(total, keep, cols), *arrays))

        early, late = give(*strips[:-1], fixed), give(strips[-1])
        edge = call(functools.partial(edge_kernel, levels), struct(count, 2, HALO, cols), *strips, fixed, early, late)
        halo = along(edge, [(1, 0, 1), (0, 1, -1)])
        high, half = HALO + keep, strip // 2
        *pieces, own, other = call(
            functools.partial(newton_kernel, levels),
            [struct(2, half, cols)] * (levels - 1) + [struct(half, cols)] * 2,
            *strips, fixed, early, late, halo,
            scratch=[pltpu.VMEM((count, 2, high, cols), jnp.float32)]
            + scratches(levels, high // SUB, cols, high),
        )
        other = swap(other)
        pieces = [pieces[0]] + [around(pieces[shift], shift) for shift in range(1, levels - 1)]
        others = [swap(call(trade_kernel, struct(levels - 1, half, cols), *pieces))]
        pieces.append(around(call(merge_kernel, struct(strip, cols), own, other), levels - 1))
    else:
        counts = [min(strip, HALO - done) for done in range(0, HALO, strip)]
        rims = call(
            functools.partial(rim_kernel, levels, counts),
            [struct(count, n, cols) for n in counts] * 2,
            *strips, fixed,
        )
        aboves = [along(rims[len(counts) + i], [(0, 0, i + 1), (1, 1, i + 1)]) for i in range(len(counts))]
        belows = [along(rims[i], [(0, 0, -i - 1), (1, 1, -i - 1)]) for i in range(len(counts))]
        high = strip + 2 * HALO
        mine = call(
            functools.partial(join_kernel, levels, counts),
            struct(count, high, cols),
            *strips, fixed, *aboves, *belows,
        )
        pieces = call(
            functools.partial(newton_wide_kernel, levels, strip),
            [struct(strip, cols)] * levels,
            mine, swap(mine),
            scratch=scratches(levels, high // SUB, cols, high),
        )
        pieces = [pieces[0]] + [around(pieces[shift], shift) for shift in range(1, levels)]
        others = []
    return call(functools.partial(place_kernel, levels, strip), struct(1, rows, cols), *pieces, *others)


def solution(mesh):
    sizes = tuple(mesh.shape[axis] for axis in ("tm", "sx", "sy"))
    in_specs = (
        P("tm", "sx", "sy"),
        P("sx", "sy"),
        P("sx", "sy"),
        P("sx", "sy"),
        P("tm", "sx", "sy"),
        P("sx", "sy"),
    )
    out_specs = P("tm", "sx", "sy")

    def whole(*args):
        return body(sizes, *args)

    return jax.shard_map(whole, mesh=mesh, in_specs=in_specs, out_specs=out_specs, check_vma=False)
```

profile of v0, /device:TPU:0, one launch (start us, length us, event | category | flops | bytes accessed | tf_op | source)
XLA Modules:
  0.0 38.2 jit_solution(1600871043312266114)
XLA Ops:
  0.0 1.2 %shard_map.64 = (f32[2,64,128]{2,1,0:T(8,128)S(1)}, f32[2,64,128]{2,1,0:T(8,128)S(1)}, f32[2,64,128]{2,1,0:T(8,128)S(1)}, f32[2,64,128]{2,1,0:T(8,128)S(1)}, f32[3,64,128]{2,1,0:T(8,128)S(1)}) custom-call(f32[1,256,128]{2,1,0:T(8,128)} %refs_0_.1, f32[1,256,128]{2,1,0:T(8,128)} %refs_1_.1, f32[256,128]{1,0:T(8,128)} %refs_2_.1, f32[256,128]{1,0:T(8,128)} %refs_3_.1, ...), custom_call_target="tpu_custom_call" | custom-call | tf_op jit(solution)/shard_map/pallas_call | solution.py:440
  1.2 3.1 %collective-permute-start = (f32[2,64,128]{2,1,0:T(8,128)S(1)}, f32[2,64,128]{2,1,0:T(8,128)S(1)}, u32[]{:S(2)}, u32[]{:S(2)}) collective-permute-start(f32[2,64,128]{2,1,0:T(8,128)S(1)} %get-tuple-element.16), channel_id=1, source_target_pairs={{0,8},{8,16},{16,24},{24,0},{1,9},{9,17},{17,25},{25,1},{2,10},{10... | collective-permute-start | bytes 196616 | tf_op jit(solution)/shard_map/ppermute | solution.py:462
  4.3 2.6 %collective-permute-start.1 = (f32[2,64,128]{2,1,0:T(8,128)S(1)}, f32[2,64,128]{2,1,0:T(8,128)S(1)}, u32[]{:S(2)}, u32[]{:S(2)}) collective-permute-start(f32[2,64,128]{2,1,0:T(8,128)S(1)} %get-tuple-element.17), channel_id=1, source_target_pairs={{0,16},{8,24},{16,0},{24,8},{1,17},{9,25},{17,1},{25,9},{2,18},{10... | collective-permute-start | bytes 196616 | tf_op jit(solution)/shard_map/ppermute | solution.py:462
  6.9 1.9 %collective-permute-done.refs_1_ = f32[2,64,128]{2,1,0:T(8,128)S(1)} collective-permute-done((f32[2,64,128]{2,1,0:T(8,128)S(1)}, f32[2,64,128]{2,1,0:T(8,128)S(1)}, u32[]{:S(2)}, u32[]{:S(2)}) %collective-permute-start) | collective-permute-done | bytes 65568 | tf_op jit(solution)/shard_map/ppermute | solution.py:462
  8.8 2.4 %collective-permute-done.1.refs_2_ = f32[2,64,128]{2,1,0:T(8,128)S(1)} collective-permute-done((f32[2,64,128]{2,1,0:T(8,128)S(1)}, f32[2,64,128]{2,1,0:T(8,128)S(1)}, u32[]{:S(2)}, u32[]{:S(2)}) %collective-permute-start.1) | collective-permute-done | bytes 65568 | tf_op jit(solution)/shard_map/ppermute | solution.py:462
  11.3 0.1 collective-permute-start.3
  11.3 2.1 %collective-permute-start.2 = (f32[2,64,128]{2,1,0:T(8,128)S(1)}, f32[2,64,128]{2,1,0:T(8,128)S(1)}, u32[]{:S(2)}, u32[]{:S(2)}) collective-permute-start(f32[2,64,128]{2,1,0:T(8,128)S(1)} %get-tuple-element.18), channel_id=1, source_target_pairs={{0,24},{8,0},{16,8},{24,16},{1,25},{9,1},{17,9},{25,17},{2,26},{10... | collective-permute-start | bytes 196616 | tf_op jit(solution)/shard_map/ppermute | solution.py:462
  13.4 2.4 %collective-permute-done.2.refs_0_.refs_3_ = f32[2,64,128]{2,1,0:T(8,128)S(1)} collective-permute-done((f32[2,64,128]{2,1,0:T(8,128)S(1)}, f32[2,64,128]{2,1,0:T(8,128)S(1)}, u32[]{:S(2)}, u32[]{:S(2)}) %collective-permute-start.2) | collective-permute-done | bytes 65568 | tf_op jit(solution)/shard_map/ppermute | solution.py:462
  15.8 0.0 collective-permute-start.4
  15.8 1.2 %collective-permute-done.4.refs_6_ = f32[2,48,128]{2,1,0:T(8,128)S(1)} collective-permute-done((f32[2,48,128]{2,1,0:T(8,128)S(1)}, f32[2,48,128]{2,1,0:T(8,128)S(1)}, u32[]{:S(2)}, u32[]{:S(2)}) %collective-permute-start.4) | collective-permute-done | bytes 49184 | tf_op jit(solution)/shard_map/ppermute | solution.py:459
  17.1 0.0 collective-permute-done.3.refs_5_
  17.1 0.7 %collective-permute-start.5 = (f32[11,2,16,128]{3,2,1,0:T(8,128)S(1)}, f32[11,2,16,128]{3,2,1,0:T(8,128)S(1)}, u32[]{:S(2)}, u32[]{:S(2)}) collective-permute-start(f32[11,2,16,128]{3,2,1,0:T(8,128)S(1)} %shard_map.67), channel_id=1, source_target_pairs={{1,8},{9,16},{8,1},{17,24},{16,9},{25,26},{24,17},{27,18},{26,25},... | collective-permute-start | bytes 540680 | tf_op jit(solution)/shard_map/ppermute | solution.py:478
  17.8 0.0 collective-permute-done.5.refs_7_
  17.8 2.5 %shard_map.68 = (f32[2,32,128]{2,1,0:T(8,128)S(1)}, f32[2,32,128]{2,1,0:T(8,128)S(1)}, f32[2,32,128]{2,1,0:T(8,128)S(1)}, f32[32,128]{1,0:T(8,128)S(1)}, f32[32,128]{1,0:T(8,128)S(1)}) custom-call(f32[2,64,128]{2,1,0:T(8,128)S(1)} %get-tuple-element.15.refs_0_, f32[2,64,128]{2,1,0:T(8,128)S(1)} %collective-permute-done.refs_1_, ...), custom_call_target="tpu_custom_call" | custom-call | tf_op jit(solution)/shard_map/pallas_call | solution.py:440
  20.3 6.2 %collective-permute-start.6 = (f32[2,32,128]{2,1,0:T(8,128)S(1)}, f32[2,32,128]{2,1,0:T(8,128)S(1)}, u32[]{:S(2)}, u32[]{:S(2)}) collective-permute-start(f32[2,32,128]{2,1,0:T(8,128)S(1)} %get-tuple-element.21), channel_id=1, source_target_pairs={{0,8},{8,16},{16,24},{24,0},{1,9},{9,17},{17,25},{25,1},{2,10},{10... | collective-permute-start | bytes 98312 | tf_op jit(solution)/shard_map/ppermute | solution.py:462
  26.5 4.3 %collective-permute-start.7 = (f32[2,32,128]{2,1,0:T(8,128)S(1)}, f32[2,32,128]{2,1,0:T(8,128)S(1)}, u32[]{:S(2)}, u32[]{:S(2)}) collective-permute-start(f32[2,32,128]{2,1,0:T(8,128)S(1)} %get-tuple-element.22), channel_id=1, source_target_pairs={{0,16},{8,24},{16,0},{24,8},{1,17},{9,25},{17,1},{25,9},{2,18},{10... | collective-permute-start | bytes 98312 | tf_op jit(solution)/shard_map/ppermute | solution.py:462
  30.9 0.0 collective-permute-start.8
  30.9 1.3 %collective-permute-done.6.refs_1_ = f32[2,32,128]{2,1,0:T(8,128)S(1)} collective-permute-done((f32[2,32,128]{2,1,0:T(8,128)S(1)}, f32[2,32,128]{2,1,0:T(8,128)S(1)}, u32[]{:S(2)}, u32[]{:S(2)}) %collective-permute-start.6) | collective-permute-done | bytes 32800 | tf_op jit(solution)/shard_map/ppermute | solution.py:462
  32.2 1.2 %collective-permute-done.7.refs_2_ = f32[2,32,128]{2,1,0:T(8,128)S(1)} collective-permute-done((f32[2,32,128]{2,1,0:T(8,128)S(1)}, f32[2,32,128]{2,1,0:T(8,128)S(1)}, u32[]{:S(2)}, u32[]{:S(2)}) %collective-permute-start.7) | collective-permute-done | bytes 32800 | tf_op jit(solution)/shard_map/ppermute | solution.py:462
  33.4 0.0 collective-permute-start.10
  33.4 0.0 collective-permute-done.8.other
  33.5 1.8 %collective-permute-start.9 = (f32[64,128]{1,0:T(8,128)S(1)}, f32[64,128]{1,0:T(8,128)S(1)}, u32[]{:S(2)}, u32[]{:S(2)}) collective-permute-start(f32[64,128]{1,0:T(8,128)S(1)} %shard_map.69), channel_id=1, source_target_pairs={{0,24},{8,0},{16,8},{24,16},{1,25},{9,1},{17,9},{25,17},{2,26},{10... | collective-permute-start | bytes 98312 | tf_op jit(solution)/shard_map/ppermute | solution.py:462
  35.3 2.1 %collective-permute-done.9.refs_3_ = f32[64,128]{1,0:T(8,128)S(1)} collective-permute-done((f32[64,128]{1,0:T(8,128)S(1)}, f32[64,128]{1,0:T(8,128)S(1)}, u32[]{:S(2)}, u32[]{:S(2)}) %collective-permute-start.9) | collective-permute-done | bytes 32800 | tf_op jit(solution)/shard_map/ppermute | solution.py:462
  37.4 0.0 collective-permute-done.10.refs_4_
  37.4 0.8 %shard_map.71 = f32[1,256,128]{2,1,0:T(8,128)} custom-call(f32[2,32,128]{2,1,0:T(8,128)S(1)} %get-tuple-element.20.refs_0_, f32[2,32,128]{2,1,0:T(8,128)S(1)} %collective-permute-done.6.refs_1_, f32[2,32,128]{2,1,0:T(8,128)S(1)} %collective-permute-done.7.refs_2_, f32[64,128]{1,0:T(8,128)S(1)} %collective-permute-done.9.refs_3_, ...), custom_call_target="tpu_custom_call" | custom-call | tf_op jit(solution)/shard_map/pallas_call | solution.py:440
  (5 shorter events, 0.1 us)
Async XLA Ops:
  1.2 7.6 %collective-permute-start = (f32[2,64,128]{2,1,0:T(8,128)S(1)}, f32[2,64,128]{2,1,0:T(8,128)S(1)}, u32[]{:S(2)}, u32[]{:S(2)}) collective-permute-start(f32[2,64,128]{2,1,0:T(8,128)S(1)} %get-tuple-element.16), channel_id=1, source_target_pairs={{0,8},{8,16},{16,24},{24,0},{1,9},{9,17},{17,25},{25,1},{2,10},{10... | collective-permute-start | bytes 196616 | tf_op jit(solution)/shard_map/ppermute | solution.py:462
  4.3 6.9 %collective-permute-start.1 = (f32[2,64,128]{2,1,0:T(8,128)S(1)}, f32[2,64,128]{2,1,0:T(8,128)S(1)}, u32[]{:S(2)}, u32[]{:S(2)}) collective-permute-start(f32[2,64,128]{2,1,0:T(8,128)S(1)} %get-tuple-element.17), channel_id=1, source_target_pairs={{0,16},{8,24},{16,0},{24,8},{1,17},{9,25},{17,1},{25,9},{2,18},{10... | collective-permute-start | bytes 196616 | tf_op jit(solution)/shard_map/ppermute | solution.py:462
  11.3 5.8 %collective-permute-start.3 = (f32[9,48,128]{2,1,0:T(8,128)S(1)}, f32[9,48,128]{2,1,0:T(8,128)S(1)}, u32[]{:S(2)}, u32[]{:S(2)}) collective-permute-start(f32[9,48,128]{2,1,0:T(8,128)S(1)} %shard_map.65), channel_id=1, source_target_pairs={{0,1},{1,0},{2,3},{3,2},{4,5},{5,4},{6,7},{7,6},{8,9},{9,8},{10,11... | collective-permute-start | bytes 663560 | tf_op jit(solution)/shard_map/ppermute | solution.py:459
  11.3 4.5 %collective-permute-start.2 = (f32[2,64,128]{2,1,0:T(8,128)S(1)}, f32[2,64,128]{2,1,0:T(8,128)S(1)}, u32[]{:S(2)}, u32[]{:S(2)}) collective-permute-start(f32[2,64,128]{2,1,0:T(8,128)S(1)} %get-tuple-element.18), channel_id=1, source_target_pairs={{0,24},{8,0},{16,8},{24,16},{1,25},{9,1},{17,9},{25,17},{2,26},{10... | collective-permute-start | bytes 196616 | tf_op jit(solution)/shard_map/ppermute | solution.py:462
  15.8 1.2 %collective-permute-start.4 = (f32[2,48,128]{2,1,0:T(8,128)S(1)}, f32[2,48,128]{2,1,0:T(8,128)S(1)}, u32[]{:S(2)}, u32[]{:S(2)}) collective-permute-start(f32[2,48,128]{2,1,0:T(8,128)S(1)} %shard_map.66), channel_id=1, source_target_pairs={{0,1},{1,0},{2,3},{3,2},{4,5},{5,4},{6,7},{7,6},{8,9},{9,8},{10,11... | collective-permute-start | bytes 147464 | tf_op jit(solution)/shard_map/ppermute | solution.py:459
  17.1 0.7 %collective-permute-start.5 = (f32[11,2,16,128]{3,2,1,0:T(8,128)S(1)}, f32[11,2,16,128]{3,2,1,0:T(8,128)S(1)}, u32[]{:S(2)}, u32[]{:S(2)}) collective-permute-start(f32[11,2,16,128]{3,2,1,0:T(8,128)S(1)} %shard_map.67), channel_id=1, source_target_pairs={{1,8},{9,16},{8,1},{17,24},{16,9},{25,26},{24,17},{27,18},{26,25},... | collective-permute-start | bytes 540680 | tf_op jit(solution)/shard_map/ppermute | solution.py:478
  20.3 11.9 %collective-permute-start.6 = (f32[2,32,128]{2,1,0:T(8,128)S(1)}, f32[2,32,128]{2,1,0:T(8,128)S(1)}, u32[]{:S(2)}, u32[]{:S(2)}) collective-permute-start(f32[2,32,128]{2,1,0:T(8,128)S(1)} %get-tuple-element.21), channel_id=1, source_target_pairs={{0,8},{8,16},{16,24},{24,0},{1,9},{9,17},{17,25},{25,1},{2,10},{10... | collective-permute-start | bytes 98312 | tf_op jit(solution)/shard_map/ppermute | solution.py:462
  26.5 6.9 %collective-permute-start.7 = (f32[2,32,128]{2,1,0:T(8,128)S(1)}, f32[2,32,128]{2,1,0:T(8,128)S(1)}, u32[]{:S(2)}, u32[]{:S(2)}) collective-permute-start(f32[2,32,128]{2,1,0:T(8,128)S(1)} %get-tuple-element.22), channel_id=1, source_target_pairs={{0,16},{8,24},{16,0},{24,8},{1,17},{9,25},{17,1},{25,9},{2,18},{10... | collective-permute-start | bytes 98312 | tf_op jit(solution)/shard_map/ppermute | solution.py:462
  30.9 2.6 %collective-permute-start.8 = (f32[32,128]{1,0:T(8,128)S(1)}, f32[32,128]{1,0:T(8,128)S(1)}, u32[]{:S(2)}, u32[]{:S(2)}) collective-permute-start(f32[32,128]{1,0:T(8,128)S(1)} %get-tuple-element.24), channel_id=1, source_target_pairs={{0,1},{1,0},{2,3},{3,2},{4,5},{5,4},{6,7},{7,6},{8,9},{9,8},{10,11... | collective-permute-start | bytes 49160 | tf_op jit(solution)/shard_map/ppermute | solution.py:459
  33.4 4.0 %collective-permute-start.10 = (f32[3,32,128]{2,1,0:T(8,128)S(1)}, f32[3,32,128]{2,1,0:T(8,128)S(1)}, u32[]{:S(2)}, u32[]{:S(2)}) collective-permute-start(f32[3,32,128]{2,1,0:T(8,128)S(1)} %shard_map.70), channel_id=1, source_target_pairs={{0,1},{1,0},{2,3},{3,2},{4,5},{5,4},{6,7},{7,6},{8,9},{9,8},{10,11... | collective-permute-start | bytes 147464 | tf_op jit(solution)/shard_map/ppermute | solution.py:459
  33.5 4.0 %collective-permute-start.9 = (f32[64,128]{1,0:T(8,128)S(1)}, f32[64,128]{1,0:T(8,128)S(1)}, u32[]{:S(2)}, u32[]{:S(2)}) collective-permute-start(f32[64,128]{1,0:T(8,128)S(1)} %shard_map.69), channel_id=1, source_target_pairs={{0,24},{8,0},{16,8},{24,16},{1,25},{9,1},{17,9},{25,17},{2,26},{10... | collective-permute-start | bytes 98312 | tf_op jit(solution)/shard_map/ppermute | solution.py:462
where the time goes:
time: 38.4 us; the launch traced here: 38.2 us
  starting transfers between devices  20.9 us (54%)
  waiting for transfers between devices  12.7 us (33%)
  Pallas kernels  4.54 us (12%)
    ppermute x6, starting transfers between devices, around(): lax.ppermute(value, 'tm', [(i, (i + shift) % levels) for i in range(level...  20.2 us
    ppermute x6, waiting for transfers between devices, around(): lax.ppermute(value, 'tm', [(i, (i + shift) % levels) for i in range(level...  11.4 us
    pallas_call x8, Pallas kernels, call(): pl.pallas_call(kernel, out_shape=outs, in_specs=[spec] * len(operands), o...  4.54 us
    ppermute x4, waiting for transfers between devices, swap(): return lax.ppermute(value, 'sy', [(0, 1), (1, 0)])  1.23 us
  transfers between devices with their start and end apart: 11, of which 7 were waited for; matrix products, arithmetic and copies ran while one was open for 0% of the time, Pallas kernels for 0%

commit v1 on v0

--- a/solution.py
+++ b/solution.py
@@ -372,8 +372,8 @@
 
 def newton_kernel(levels, *refs):
     strips, fixed, early, late, halo = refs[:levels], *refs[levels : levels + 4]
-    outs = refs[levels + 4 : 2 * levels + 5]
-    window, spaces = refs[2 * levels + 5], refs[2 * levels + 6 :]
+    spaces = refs[levels + 4 :]
+    outs, window, spaces = spaces[: levels - ahead(levels) + 2], spaces[levels - ahead(levels) + 2], spaces[levels - ahead(levels) + 3 :]
     strip, keep = fixed.shape[1], late.shape[1]
     me, part = lax.axis_index("tm"), lax.axis_index("sy")
     depth = (HALO + keep) // SUB
@@ -383,13 +383,15 @@
     lay(levels, window.at[:, 0], rows, strips, fixed, pl.ds(aligned(part * (strip - keep)), keep))
     plain = newton_steps(levels, lambda field, half, q: window[field, half, pl.ds(q, SUB, stride=depth), :], spaces)
     first = aligned(HALO + part * (keep - strip // 2))
+    early = levels - ahead(levels)
+    own, other = outs[early:]
     for shift in range(levels):
         target = lax.rem(me + shift, levels)
-        if shift < levels - 1:
+        if shift < early:
             outs[shift][...] = plain[target, :, pl.ds(first, strip // 2)]
         else:
-            outs[shift][...] = plain[target, 0, pl.ds(first, strip // 2)]
-            outs[shift + 1][...] = plain[target, 1, pl.ds(first, strip // 2)]
+            own[shift - early] = plain[target, 0, pl.ds(first, strip // 2)]
+            other[shift - early] = plain[target, 1, pl.ds(first, strip // 2)]
 
 
 def newton_wide_kernel(levels, strip, *refs):
@@ -402,11 +404,16 @@
         outs[shift][...] = plain[target, 0, HALO : HALO + strip]
 
 
-def merge_kernel(own, other, out):
-    half = own.shape[0]
+def ahead(levels):
+    return max(1, levels // 2)
+
+
+def merge_kernel(own, other, *outs):
+    half = own.shape[1]
     part = lax.axis_index("sy")
-    out[pl.ds(aligned(part * half), half)] = own[...]
-    out[pl.ds(aligned((1 - part) * half), half)] = other[...]
+    for index, out in enumerate(outs):
+        out[pl.ds(aligned(part * half), half)] = own[index]
+        out[pl.ds(aligned((1 - part) * half), half)] = other[index]
 
 
 def trade_kernel(*refs):
@@ -428,7 +435,7 @@
 
     for shift in range(levels):
         first = strip_of(levels, level_of(levels, shift)) * strip
-        if others and shift < levels - 1:
+        if others and shift < levels - ahead(levels):
             half = strip // 2
             put(first + part * half, pieces[shift].at[0])
             put(first + (1 - part) * half, others[0].at[shift])
@@ -497,21 +504,23 @@
             total = sum(array.shape[0] for array in arrays)
             return swap(call(give_kernel, struct(total, keep, cols), *arrays))
 
-        early, late = give(*strips[:-1], fixed), give(strips[-1])
-        edge = call(functools.partial(edge_kernel, levels), struct(count, 2, HALO, cols), *strips, fixed, early, late)
+        first, second = give(*strips[:-1], fixed), give(strips[-1])
+        edge = call(functools.partial(edge_kernel, levels), struct(count, 2, HALO, cols), *strips, fixed, first, second)
         halo = along(edge, [(1, 0, 1), (0, 1, -1)])
-        high, half = HALO + keep, strip // 2
+        high, half, late = HALO + keep, strip // 2, ahead(levels)
         *pieces, own, other = call(
             functools.partial(newton_kernel, levels),
-            [struct(2, half, cols)] * (levels - 1) + [struct(half, cols)] * 2,
-            *strips, fixed, early, late, halo,
+            [struct(2, half, cols)] * (levels - late) + [struct(late, half, cols)] * 2,
+            *strips, fixed, first, second, halo,
             scratch=[pltpu.VMEM((count, 2, high, cols), jnp.float32)]
             + scratches(levels, high // SUB, cols, high),
         )
         other = swap(other)
-        pieces = [pieces[0]] + [around(pieces[shift], shift) for shift in range(1, levels - 1)]
-        others = [swap(call(trade_kernel, struct(levels - 1, half, cols), *pieces))]
-        pieces.append(around(call(merge_kernel, struct(strip, cols), own, other), levels - 1))
+        early = levels - late
+        pieces = [pieces[0]] + [around(pieces[shift], shift) for shift in range(1, early)]
+        others = [swap(call(trade_kernel, struct(early, half, cols), *pieces))]
+        merged = call(merge_kernel, [struct(strip, cols)] * late, own, other)
+        pieces += [around(piece, shift) for shift, piece in enumerate(merged, early)]
     else:
         counts = [min(strip, HALO - done) for done in range(0, HALO, strip)]
         rims = call(

time: 38.4 us -> 38.4 us (level)
  waiting for transfers between devices: 12.7 us -> 16.5 us
  starting transfers between devices: 20.9 us -> 17.1 us
    ppermute x6, starting transfers between devices: 20.2 us -> 16.1 us  [around(): lax.ppermute(value, 'tm', [(i, (i + shift) % levels) for i in range(level...]
    ppermute x6, waiting for transfers between devices: 11.4 us -> 15.3 us  [around(): lax.ppermute(value, 'tm', [(i, (i + shift) % levels) for i in range(level...]
where the time goes in v1:
time: 38.4 us; the launch traced here: 38.2 us
  starting transfers between devices  17.1 us (45%)
  waiting for transfers between devices  16.5 us (43%)
  Pallas kernels  4.53 us (12%)
    ppermute x6, starting transfers between devices, around(): lax.ppermute(value, 'tm', [(i, (i + shift) % levels) for i in range(level...  16.1 us
    ppermute x6, waiting for transfers between devices, around(): lax.ppermute(value, 'tm', [(i, (i + shift) % levels) for i in range(level...  15.3 us
    pallas_call x8, Pallas kernels, call(): pl.pallas_call(kernel, out_shape=outs, in_specs=[spec] * len(operands), o...  4.53 us
    ppermute x4, waiting for transfers between devices, swap(): return lax.ppermute(value, 'sy', [(0, 1), (1, 0)])  1.23 us
  transfers between devices with their start and end apart: 11, of which 7 were waited for; matrix products, arithmetic and copies ran while one was open for 0% of the time, Pallas kernels for 0%

profile of v1, /device:TPU:0, one launch (start us, length us, event | category | flops | bytes accessed | tf_op | source)
XLA Modules:
  0.0 38.2 jit_solution(12563561697792556135)
XLA Ops:
  0.0 1.2 %shard_map.64 = (f32[2,64,128]{2,1,0:T(8,128)S(1)}, f32[2,64,128]{2,1,0:T(8,128)S(1)}, f32[2,64,128]{2,1,0:T(8,128)S(1)}, f32[2,64,128]{2,1,0:T(8,128)S(1)}, f32[3,64,128]{2,1,0:T(8,128)S(1)}) custom-call(f32[1,256,128]{2,1,0:T(8,128)} %refs_0_.1, f32[1,256,128]{2,1,0:T(8,128)} %refs_1_.1, f32[256,128]{1,0:T(8,128)} %refs_2_.1, f32[256,128]{1,0:T(8,128)} %refs_3_.1, ...), custom_call_target="tpu_custom_call" | custom-call | tf_op jit(solution)/shard_map/pallas_call | solution.py:447
  1.2 3.1 %collective-permute-start = (f32[2,64,128]{2,1,0:T(8,128)S(1)}, f32[2,64,128]{2,1,0:T(8,128)S(1)}, u32[]{:S(2)}, u32[]{:S(2)}) collective-permute-start(f32[2,64,128]{2,1,0:T(8,128)S(1)} %get-tuple-element.17), channel_id=1, source_target_pairs={{0,8},{8,16},{16,24},{24,0},{1,9},{9,17},{17,25},{25,1},{2,10},{10... | collective-permute-start | bytes 196616 | tf_op jit(solution)/shard_map/ppermute | solution.py:469
  4.3 2.6 %collective-permute-start.1 = (f32[2,64,128]{2,1,0:T(8,128)S(1)}, f32[2,64,128]{2,1,0:T(8,128)S(1)}, u32[]{:S(2)}, u32[]{:S(2)}) collective-permute-start(f32[2,64,128]{2,1,0:T(8,128)S(1)} %get-tuple-element.18), channel_id=1, source_target_pairs={{0,16},{8,24},{16,0},{24,8},{1,17},{9,25},{17,1},{25,9},{2,18},{10... | collective-permute-start | bytes 196616 | tf_op jit(solution)/shard_map/ppermute | solution.py:469
  6.9 1.9 %collective-permute-done.refs_1_ = f32[2,64,128]{2,1,0:T(8,128)S(1)} collective-permute-done((f32[2,64,128]{2,1,0:T(8,128)S(1)}, f32[2,64,128]{2,1,0:T(8,128)S(1)}, u32[]{:S(2)}, u32[]{:S(2)}) %collective-permute-start) | collective-permute-done | bytes 65568 | tf_op jit(solution)/shard_map/ppermute | solution.py:469
  8.8 2.4 %collective-permute-done.1.refs_2_ = f32[2,64,128]{2,1,0:T(8,128)S(1)} collective-permute-done((f32[2,64,128]{2,1,0:T(8,128)S(1)}, f32[2,64,128]{2,1,0:T(8,128)S(1)}, u32[]{:S(2)}, u32[]{:S(2)}) %collective-permute-start.1) | collective-permute-done | bytes 65568 | tf_op jit(solution)/shard_map/ppermute | solution.py:469
  11.3 0.1 collective-permute-start.3
  11.3 2.1 %collective-permute-start.2 = (f32[2,64,128]{2,1,0:T(8,128)S(1)}, f32[2,64,128]{2,1,0:T(8,128)S(1)}, u32[]{:S(2)}, u32[]{:S(2)}) collective-permute-start(f32[2,64,128]{2,1,0:T(8,128)S(1)} %get-tuple-element.19), channel_id=1, source_target_pairs={{0,24},{8,0},{16,8},{24,16},{1,25},{9,1},{17,9},{25,17},{2,26},{10... | collective-permute-start | bytes 196616 | tf_op jit(solution)/shard_map/ppermute | solution.py:469
  13.4 2.4 %collective-permute-done.2.refs_0_.refs_3_ = f32[2,64,128]{2,1,0:T(8,128)S(1)} collective-permute-done((f32[2,64,128]{2,1,0:T(8,128)S(1)}, f32[2,64,128]{2,1,0:T(8,128)S(1)}, u32[]{:S(2)}, u32[]{:S(2)}) %collective-permute-start.2) | collective-permute-done | bytes 65568 | tf_op jit(solution)/shard_map/ppermute | solution.py:469
  15.8 0.0 collective-permute-start.4
  15.8 1.2 %collective-permute-done.4.refs_6_ = f32[2,48,128]{2,1,0:T(8,128)S(1)} collective-permute-done((f32[2,48,128]{2,1,0:T(8,128)S(1)}, f32[2,48,128]{2,1,0:T(8,128)S(1)}, u32[]{:S(2)}, u32[]{:S(2)}) %collective-permute-start.4) | collective-permute-done | bytes 49184 | tf_op jit(solution)/shard_map/ppermute | solution.py:466
  17.1 0.0 collective-permute-done.3.refs_5_
  17.1 0.7 %collective-permute-start.5 = (f32[11,2,16,128]{3,2,1,0:T(8,128)S(1)}, f32[11,2,16,128]{3,2,1,0:T(8,128)S(1)}, u32[]{:S(2)}, u32[]{:S(2)}) collective-permute-start(f32[11,2,16,128]{3,2,1,0:T(8,128)S(1)} %shard_map.67), channel_id=1, source_target_pairs={{1,8},{9,16},{8,1},{17,24},{16,9},{25,26},{24,17},{27,18},{26,25},... | collective-permute-start | bytes 540680 | tf_op jit(solution)/shard_map/ppermute | solution.py:485
  17.8 0.0 collective-permute-done.5.refs_7_
  17.8 2.5 %shard_map.68 = (f32[2,32,128]{2,1,0:T(8,128)S(1)}, f32[2,32,128]{2,1,0:T(8,128)S(1)}, f32[2,32,128]{2,1,0:T(8,128)S(1)}, f32[2,32,128]{2,1,0:T(8,128)S(1)}) custom-call(f32[2,64,128]{2,1,0:T(8,128)S(1)} %get-tuple-element.16.refs_0_, f32[2,64,128]{2,1,0:T(8,128)S(1)} %collective-permute-done.refs_1_, f32[2,64,128]{2,1,0:T(8,128)S(1)} %collective-permute-done.1.refs_2_, ...), custom_call_target="tpu_custom_call" | custom-call | tf_op jit(solution)/shard_map/pallas_call | solution.py:447
  20.3 6.2 %collective-permute-start.6 = (f32[2,32,128]{2,1,0:T(8,128)S(1)}, f32[2,32,128]{2,1,0:T(8,128)S(1)}, u32[]{:S(2)}, u32[]{:S(2)}) collective-permute-start(f32[2,32,128]{2,1,0:T(8,128)S(1)} %get-tuple-element.22), channel_id=1, source_target_pairs={{0,8},{8,16},{16,24},{24,0},{1,9},{9,17},{17,25},{25,1},{2,10},{10... | collective-permute-start | bytes 98312 | tf_op jit(solution)/shard_map/ppermute | solution.py:469
  26.5 0.2 collective-permute-start.7
  26.7 5.5 %collective-permute-done.6.refs_1_ = f32[2,32,128]{2,1,0:T(8,128)S(1)} collective-permute-done((f32[2,32,128]{2,1,0:T(8,128)S(1)}, f32[2,32,128]{2,1,0:T(8,128)S(1)}, u32[]{:S(2)}, u32[]{:S(2)}) %collective-permute-start.6) | collective-permute-done | bytes 32800 | tf_op jit(solution)/shard_map/ppermute | solution.py:469
  32.2 0.0 collective-permute-start.10
  32.2 0.0 collective-permute-done.7.other
  32.2 0.3 collective-permute-start.8
  32.6 1.8 %collective-permute-start.9 = (f32[64,128]{1,0:T(8,128)S(1)}, f32[64,128]{1,0:T(8,128)S(1)}, u32[]{:S(2)}, u32[]{:S(2)}) collective-permute-start(f32[64,128]{1,0:T(8,128)S(1)} %get-tuple-element.26), channel_id=1, source_target_pairs={{0,24},{8,0},{16,8},{24,16},{1,25},{9,1},{17,9},{25,17},{2,26},{10... | collective-permute-start | bytes 98312 | tf_op jit(solution)/shard_map/ppermute | solution.py:469
  34.4 0.0 collective-permute-done.10.refs_4_
  34.4 2.8 %collective-permute-done.8.refs_2_ = f32[64,128]{1,0:T(8,128)S(1)} collective-permute-done((f32[64,128]{1,0:T(8,128)S(1)}, f32[64,128]{1,0:T(8,128)S(1)}, u32[]{:S(2)}, u32[]{:S(2)}) %collective-permute-start.8) | collective-permute-done | bytes 32800 | tf_op jit(solution)/shard_map/ppermute | solution.py:469
  37.2 0.3 collective-permute-done.9.refs_3_
  37.4 0.8 %shard_map.71 = f32[1,256,128]{2,1,0:T(8,128)} custom-call(f32[2,32,128]{2,1,0:T(8,128)S(1)} %get-tuple-element.21.refs_0_, f32[2,32,128]{2,1,0:T(8,128)S(1)} %collective-permute-done.6.refs_1_, f32[64,128]{1,0:T(8,128)S(1)} %collective-permute-done.8.refs_2_, f32[64,128]{1,0:T(8,128)S(1)} %collective-permute-done.9.refs_3_, ...), custom_call_target="tpu_custom_call" | custom-call | tf_op jit(solution)/shard_map/pallas_call | solution.py:447
  (5 shorter events, 0.1 us)
Async XLA Ops:
  1.2 7.6 %collective-permute-start = (f32[2,64,128]{2,1,0:T(8,128)S(1)}, f32[2,64,128]{2,1,0:T(8,128)S(1)}, u32[]{:S(2)}, u32[]{:S(2)}) collective-permute-start(f32[2,64,128]{2,1,0:T(8,128)S(1)} %get-tuple-element.17), channel_id=1, source_target_pairs={{0,8},{8,16},{16,24},{24,0},{1,9},{9,17},{17,25},{25,1},{2,10},{10... | collective-permute-start | bytes 196616 | tf_op jit(solution)/shard_map/ppermute | solution.py:469
  4.3 6.9 %collective-permute-start.1 = (f32[2,64,128]{2,1,0:T(8,128)S(1)}, f32[2,64,128]{2,1,0:T(8,128)S(1)}, u32[]{:S(2)}, u32[]{:S(2)}) collective-permute-start(f32[2,64,128]{2,1,0:T(8,128)S(1)} %get-tuple-element.18), channel_id=1, source_target_pairs={{0,16},{8,24},{16,0},{24,8},{1,17},{9,25},{17,1},{25,9},{2,18},{10... | collective-permute-start | bytes 196616 | tf_op jit(solution)/shard_map/ppermute | solution.py:469
  11.3 5.8 %collective-permute-start.3 = (f32[9,48,128]{2,1,0:T(8,128)S(1)}, f32[9,48,128]{2,1,0:T(8,128)S(1)}, u32[]{:S(2)}, u32[]{:S(2)}) collective-permute-start(f32[9,48,128]{2,1,0:T(8,128)S(1)} %shard_map.65), channel_id=1, source_target_pairs={{0,1},{1,0},{2,3},{3,2},{4,5},{5,4},{6,7},{7,6},{8,9},{9,8},{10,11... | collective-permute-start | bytes 663560 | tf_op jit(solution)/shard_map/ppermute | solution.py:466
  11.3 4.5 %collective-permute-start.2 = (f32[2,64,128]{2,1,0:T(8,128)S(1)}, f32[2,64,128]{2,1,0:T(8,128)S(1)}, u32[]{:S(2)}, u32[]{:S(2)}) collective-permute-start(f32[2,64,128]{2,1,0:T(8,128)S(1)} %get-tuple-element.19), channel_id=1, source_target_pairs={{0,24},{8,0},{16,8},{24,16},{1,25},{9,1},{17,9},{25,17},{2,26},{10... | collective-permute-start | bytes 196616 | tf_op jit(solution)/shard_map/ppermute | solution.py:469
  15.8 1.2 %collective-permute-start.4 = (f32[2,48,128]{2,1,0:T(8,128)S(1)}, f32[2,48,128]{2,1,0:T(8,128)S(1)}, u32[]{:S(2)}, u32[]{:S(2)}) collective-permute-start(f32[2,48,128]{2,1,0:T(8,128)S(1)} %shard_map.66), channel_id=1, source_target_pairs={{0,1},{1,0},{2,3},{3,2},{4,5},{5,4},{6,7},{7,6},{8,9},{9,8},{10,11... | collective-permute-start | bytes 147464 | tf_op jit(solution)/shard_map/ppermute | solution.py:466
  17.1 0.7 %collective-permute-start.5 = (f32[11,2,16,128]{3,2,1,0:T(8,128)S(1)}, f32[11,2,16,128]{3,2,1,0:T(8,128)S(1)}, u32[]{:S(2)}, u32[]{:S(2)}) collective-permute-start(f32[11,2,16,128]{3,2,1,0:T(8,128)S(1)} %shard_map.67), channel_id=1, source_target_pairs={{1,8},{9,16},{8,1},{17,24},{16,9},{25,26},{24,17},{27,18},{26,25},... | collective-permute-start | bytes 540680 | tf_op jit(solution)/shard_map/ppermute | solution.py:485
  20.3 11.9 %collective-permute-start.6 = (f32[2,32,128]{2,1,0:T(8,128)S(1)}, f32[2,32,128]{2,1,0:T(8,128)S(1)}, u32[]{:S(2)}, u32[]{:S(2)}) collective-permute-start(f32[2,32,128]{2,1,0:T(8,128)S(1)} %get-tuple-element.22), channel_id=1, source_target_pairs={{0,8},{8,16},{16,24},{24,0},{1,9},{9,17},{17,25},{25,1},{2,10},{10... | collective-permute-start | bytes 98312 | tf_op jit(solution)/shard_map/ppermute | solution.py:469
  26.5 5.7 %collective-permute-start.7 = (f32[2,32,128]{2,1,0:T(8,128)S(1)}, f32[2,32,128]{2,1,0:T(8,128)S(1)}, u32[]{:S(2)}, u32[]{:S(2)}) collective-permute-start(f32[2,32,128]{2,1,0:T(8,128)S(1)} %get-tuple-element.24), channel_id=1, source_target_pairs={{0,1},{1,0},{2,3},{3,2},{4,5},{5,4},{6,7},{7,6},{8,9},{9,8},{10,11... | collective-permute-start | bytes 98312 | tf_op jit(solution)/shard_map/ppermute | solution.py:466
  32.2 2.2 %collective-permute-start.10 = (f32[2,32,128]{2,1,0:T(8,128)S(1)}, f32[2,32,128]{2,1,0:T(8,128)S(1)}, u32[]{:S(2)}, u32[]{:S(2)}) collective-permute-start(f32[2,32,128]{2,1,0:T(8,128)S(1)} %shard_map.70), channel_id=1, source_target_pairs={{0,1},{1,0},{2,3},{3,2},{4,5},{5,4},{6,7},{7,6},{8,9},{9,8},{10,11... | collective-permute-start | bytes 98312 | tf_op jit(solution)/shard_map/ppermute | solution.py:466
  32.2 4.9 %collective-permute-start.8 = (f32[64,128]{1,0:T(8,128)S(1)}, f32[64,128]{1,0:T(8,128)S(1)}, u32[]{:S(2)}, u32[]{:S(2)}) collective-permute-start(f32[64,128]{1,0:T(8,128)S(1)} %get-tuple-element.25), channel_id=1, source_target_pairs={{0,16},{8,24},{16,0},{24,8},{1,17},{9,25},{17,1},{25,9},{2,18},{10... | collective-permute-start | bytes 98312 | tf_op jit(solution)/shard_map/ppermute | solution.py:469
  32.6 4.9 %collective-permute-start.9 = (f32[64,128]{1,0:T(8,128)S(1)}, f32[64,128]{1,0:T(8,128)S(1)}, u32[]{:S(2)}, u32[]{:S(2)}) collective-permute-start(f32[64,128]{1,0:T(8,128)S(1)} %get-tuple-element.26), channel_id=1, source_target_pairs={{0,24},{8,0},{16,8},{24,16},{1,25},{9,1},{17,9},{25,17},{2,26},{10... | collective-permute-start | bytes 98312 | tf_op jit(solution)/shard_map/ppermute | solution.py:469

commit v2 on v1

--- a/solution.py
+++ b/solution.py
@@ -37,6 +37,10 @@
     return jnp.where(lax.rem(lax.axis_index("sx"), 2) == 0, tm, levels - 1 - tm)
 
 
+def way_out(levels):
+    return [*range(levels - 2), levels - 1, levels - 2] if levels > 2 else list(range(levels))
+
+
 def level_of(levels, shift):
     return lax.rem(lax.axis_index("tm") + levels - shift, levels)
 
@@ -56,7 +60,7 @@
 
     copies = []
     for shift in range(levels):
-        here = rows_of(lax.rem(me + shift, levels))
+        here = rows_of(lax.rem(me + way_out(levels)[shift], levels))
         copies += [(guess.at[0, here], strips[shift].at[0]), (balance.at[0, here], strips[shift].at[1])]
     here = rows_of(me)
     copies += [
@@ -82,8 +86,8 @@
 
 
 def lay(levels, out, rows, strips, fixed, source):
-    for shift in range(levels):
-        level = level_of(levels, shift)
+    for shift, hops in enumerate(way_out(levels)):
+        level = level_of(levels, hops)
         out[level, rows] = strips[shift][0, source]
         out[levels + level, rows] = strips[shift][1, source]
     out[2 * levels :, rows] = fixed[:, source]
@@ -100,8 +104,8 @@
 
 
 def lay_taken(levels, out, index, early, late, source):
-    for shift in range(levels):
-        level = level_of(levels, shift)
+    for shift, hops in enumerate(way_out(levels)):
+        level = level_of(levels, hops)
         ref, place = (early, 2 * shift) if shift < levels - 1 else (late, 0)
         out[(level, *index)] = ref[place, source]
         out[(levels + level, *index)] = ref[place + 1, source]
@@ -497,7 +501,8 @@
         params=fetching,
     )
     strips, fixed = packed[:levels], packed[levels]
-    strips = [strips[0]] + [around(strips[shift], shift) for shift in range(1, levels)]
+    hops = way_out(levels)
+    strips = [strips[0]] + [around(strips[turn], hops[turn]) for turn in range(1, levels)]
 
     if strip % (2 * SUB) == 0 and keep <= strip:
         def give(*arrays):

time: 38.4 us -> 38.1 us (level)
  starting transfers between devices: 17.1 us -> 16.3 us
    ppermute x6, starting transfers between devices: 16.1 us -> 15.3 us  [around(): lax.ppermute(value, 'tm', [(i, (i + shift) % levels) for i in range(level...]
  transfers between devices with their start and end apart: 11 -> 11, of which waited for: 7 -> 6; matrix products, arithmetic and copies ran while one was open for 0% -> 0% of each run, Pallas kernels for 0% -> 0%
where the time goes in v2:
time: 38.1 us; the launch traced here: 37.6 us
  waiting for transfers between devices  16.7 us (44%)
  starting transfers between devices  16.3 us (43%)
  Pallas kernels  4.53 us (12%)
    ppermute x6, waiting for transfers between devices, around(): lax.ppermute(value, 'tm', [(i, (i + shift) % levels) for i in range(level...  15.5 us
    ppermute x6, starting transfers between devices, around(): lax.ppermute(value, 'tm', [(i, (i + shift) % levels) for i in range(level...  15.3 us
    pallas_call x8, Pallas kernels, call(): pl.pallas_call(kernel, out_shape=outs, in_specs=[spec] * len(operands), o...  4.53 us
    ppermute x4, waiting for transfers between devices, swap(): return lax.ppermute(value, 'sy', [(0, 1), (1, 0)])  1.23 us
  transfers between devices with their start and end apart: 11, of which 6 were waited for; matrix products, arithmetic and copies ran while one was open for 0% of the time, Pallas kernels for 0%

profile of v2, /device:TPU:0, one launch (start us, length us, event | category | flops | bytes accessed | tf_op | source)
XLA Modules:
  0.0 37.6 jit_solution(4016354098921352261)
XLA Ops:
  0.0 1.2 %shard_map.64 = (f32[2,64,128]{2,1,0:T(8,128)S(1)}, f32[2,64,128]{2,1,0:T(8,128)S(1)}, f32[2,64,128]{2,1,0:T(8,128)S(1)}, f32[2,64,128]{2,1,0:T(8,128)S(1)}, f32[3,64,128]{2,1,0:T(8,128)S(1)}) custom-call(f32[1,256,128]{2,1,0:T(8,128)} %refs_0_.1, f32[1,256,128]{2,1,0:T(8,128)} %refs_1_.1, f32[256,128]{1,0:T(8,128)} %refs_2_.1, f32[256,128]{1,0:T(8,128)} %refs_3_.1, ...), custom_call_target="tpu_custom_call" | custom-call | tf_op jit(solution)/shard_map/pallas_call | solution.py:451
  1.2 3.1 %collective-permute-start = (f32[2,64,128]{2,1,0:T(8,128)S(1)}, f32[2,64,128]{2,1,0:T(8,128)S(1)}, u32[]{:S(2)}, u32[]{:S(2)}) collective-permute-start(f32[2,64,128]{2,1,0:T(8,128)S(1)} %get-tuple-element.17), channel_id=1, source_target_pairs={{0,8},{8,16},{16,24},{24,0},{1,9},{9,17},{17,25},{25,1},{2,10},{10... | collective-permute-start | bytes 196616 | tf_op jit(solution)/shard_map/ppermute | solution.py:473
  4.3 2.1 %collective-permute-start.1 = (f32[2,64,128]{2,1,0:T(8,128)S(1)}, f32[2,64,128]{2,1,0:T(8,128)S(1)}, u32[]{:S(2)}, u32[]{:S(2)}) collective-permute-start(f32[2,64,128]{2,1,0:T(8,128)S(1)} %get-tuple-element.18), channel_id=1, source_target_pairs={{0,24},{8,0},{16,8},{24,16},{1,25},{9,1},{17,9},{25,17},{2,26},{10... | collective-permute-start | bytes 196616 | tf_op jit(solution)/shard_map/ppermute | solution.py:473
  6.4 2.3 %collective-permute-done.refs_1_ = f32[2,64,128]{2,1,0:T(8,128)S(1)} collective-permute-done((f32[2,64,128]{2,1,0:T(8,128)S(1)}, f32[2,64,128]{2,1,0:T(8,128)S(1)}, u32[]{:S(2)}, u32[]{:S(2)}) %collective-permute-start) | collective-permute-done | bytes 65568 | tf_op jit(solution)/shard_map/ppermute | solution.py:473
  8.7 0.6 %collective-permute-done.1.refs_2_ = f32[2,64,128]{2,1,0:T(8,128)S(1)} collective-permute-done((f32[2,64,128]{2,1,0:T(8,128)S(1)}, f32[2,64,128]{2,1,0:T(8,128)S(1)}, u32[]{:S(2)}, u32[]{:S(2)}) %collective-permute-start.1) | collective-permute-done | bytes 65568 | tf_op jit(solution)/shard_map/ppermute | solution.py:473
  9.3 0.1 collective-permute-start.3
  9.4 2.0 %collective-permute-start.2 = (f32[2,64,128]{2,1,0:T(8,128)S(1)}, f32[2,64,128]{2,1,0:T(8,128)S(1)}, u32[]{:S(2)}, u32[]{:S(2)}) collective-permute-start(f32[2,64,128]{2,1,0:T(8,128)S(1)} %get-tuple-element.19), channel_id=1, source_target_pairs={{0,16},{8,24},{16,0},{24,8},{1,17},{9,25},{17,1},{25,9},{2,18},{10... | collective-permute-start | bytes 196616 | tf_op jit(solution)/shard_map/ppermute | solution.py:473
  11.3 4.8 %collective-permute-done.2.refs_0_.refs_3_ = f32[2,64,128]{2,1,0:T(8,128)S(1)} collective-permute-done((f32[2,64,128]{2,1,0:T(8,128)S(1)}, f32[2,64,128]{2,1,0:T(8,128)S(1)}, u32[]{:S(2)}, u32[]{:S(2)}) %collective-permute-start.2) | collective-permute-done | bytes 65568 | tf_op jit(solution)/shard_map/ppermute | solution.py:473
  16.2 0.0 collective-permute-start.4
  16.2 1.2 %collective-permute-done.4.refs_6_ = f32[2,48,128]{2,1,0:T(8,128)S(1)} collective-permute-done((f32[2,48,128]{2,1,0:T(8,128)S(1)}, f32[2,48,128]{2,1,0:T(8,128)S(1)}, u32[]{:S(2)}, u32[]{:S(2)}) %collective-permute-start.4) | collective-permute-done | bytes 49184 | tf_op jit(solution)/shard_map/ppermute | solution.py:470
  17.4 0.0 collective-permute-done.3.refs_5_
  17.4 0.7 %collective-permute-start.5 = (f32[11,2,16,128]{3,2,1,0:T(8,128)S(1)}, f32[11,2,16,128]{3,2,1,0:T(8,128)S(1)}, u32[]{:S(2)}, u32[]{:S(2)}) collective-permute-start(f32[11,2,16,128]{3,2,1,0:T(8,128)S(1)} %shard_map.67), channel_id=1, source_target_pairs={{1,8},{9,16},{8,1},{17,24},{16,9},{25,26},{24,17},{27,18},{26,25},... | collective-permute-start | bytes 540680 | tf_op jit(solution)/shard_map/ppermute | solution.py:489
  18.1 0.0 collective-permute-done.5.refs_7_
  18.1 2.5 %shard_map.68 = (f32[2,32,128]{2,1,0:T(8,128)S(1)}, f32[2,32,128]{2,1,0:T(8,128)S(1)}, f32[2,32,128]{2,1,0:T(8,128)S(1)}, f32[2,32,128]{2,1,0:T(8,128)S(1)}) custom-call(f32[2,64,128]{2,1,0:T(8,128)S(1)} %get-tuple-element.16.refs_0_, f32[2,64,128]{2,1,0:T(8,128)S(1)} %collective-permute-done.refs_1_, f32[2,64,128]{2,1,0:T(8,128)S(1)} %collective-permute-done.1.refs_2_, ...), custom_call_target="tpu_custom_call" | custom-call | tf_op jit(solution)/shard_map/pallas_call | solution.py:451
  20.7 6.2 %collective-permute-start.6 = (f32[2,32,128]{2,1,0:T(8,128)S(1)}, f32[2,32,128]{2,1,0:T(8,128)S(1)}, u32[]{:S(2)}, u32[]{:S(2)}) collective-permute-start(f32[2,32,128]{2,1,0:T(8,128)S(1)} %get-tuple-element.22), channel_id=1, source_target_pairs={{0,8},{8,16},{16,24},{24,0},{1,9},{9,17},{17,25},{25,1},{2,10},{10... | collective-permute-start | bytes 98312 | tf_op jit(solution)/shard_map/ppermute | solution.py:473
  26.9 0.2 collective-permute-start.7
  27.1 4.6 %collective-permute-done.6.refs_1_ = f32[2,32,128]{2,1,0:T(8,128)S(1)} collective-permute-done((f32[2,32,128]{2,1,0:T(8,128)S(1)}, f32[2,32,128]{2,1,0:T(8,128)S(1)}, u32[]{:S(2)}, u32[]{:S(2)}) %collective-permute-start.6) | collective-permute-done | bytes 32800 | tf_op jit(solution)/shard_map/ppermute | solution.py:473
  31.6 0.1 collective-permute-start.10
  31.8 0.0 collective-permute-done.7.other
  31.8 0.1 collective-permute-start.8
  31.9 1.8 %collective-permute-start.9 = (f32[64,128]{1,0:T(8,128)S(1)}, f32[64,128]{1,0:T(8,128)S(1)}, u32[]{:S(2)}, u32[]{:S(2)}) collective-permute-start(f32[64,128]{1,0:T(8,128)S(1)} %get-tuple-element.26), channel_id=1, source_target_pairs={{0,24},{8,0},{16,8},{24,16},{1,25},{9,1},{17,9},{25,17},{2,26},{10... | collective-permute-start | bytes 98312 | tf_op jit(solution)/shard_map/ppermute | solution.py:473
  33.7 0.0 collective-permute-done.10.refs_4_
  33.7 3.2 %collective-permute-done.8.refs_2_ = f32[64,128]{1,0:T(8,128)S(1)} collective-permute-done((f32[64,128]{1,0:T(8,128)S(1)}, f32[64,128]{1,0:T(8,128)S(1)}, u32[]{:S(2)}, u32[]{:S(2)}) %collective-permute-start.8) | collective-permute-done | bytes 32800 | tf_op jit(solution)/shard_map/ppermute | solution.py:473
  36.9 0.0 collective-permute-done.9.refs_3_
  36.9 0.8 %shard_map.71 = f32[1,256,128]{2,1,0:T(8,128)} custom-call(f32[2,32,128]{2,1,0:T(8,128)S(1)} %get-tuple-element.21.refs_0_, f32[2,32,128]{2,1,0:T(8,128)S(1)} %collective-permute-done.6.refs_1_, f32[64,128]{1,0:T(8,128)S(1)} %collective-permute-done.8.refs_2_, f32[64,128]{1,0:T(8,128)S(1)} %collective-permute-done.9.refs_3_, ...), custom_call_target="tpu_custom_call" | custom-call | tf_op jit(solution)/shard_map/pallas_call | solution.py:451
  (5 shorter events, 0.0 us)
Async XLA Ops:
  1.2 7.5 %collective-permute-start = (f32[2,64,128]{2,1,0:T(8,128)S(1)}, f32[2,64,128]{2,1,0:T(8,128)S(1)}, u32[]{:S(2)}, u32[]{:S(2)}) collective-permute-start(f32[2,64,128]{2,1,0:T(8,128)S(1)} %get-tuple-element.17), channel_id=1, source_target_pairs={{0,8},{8,16},{16,24},{24,0},{1,9},{9,17},{17,25},{25,1},{2,10},{10... | collective-permute-start | bytes 196616 | tf_op jit(solution)/shard_map/ppermute | solution.py:473
  4.3 5.0 %collective-permute-start.1 = (f32[2,64,128]{2,1,0:T(8,128)S(1)}, f32[2,64,128]{2,1,0:T(8,128)S(1)}, u32[]{:S(2)}, u32[]{:S(2)}) collective-permute-start(f32[2,64,128]{2,1,0:T(8,128)S(1)} %get-tuple-element.18), channel_id=1, source_target_pairs={{0,24},{8,0},{16,8},{24,16},{1,25},{9,1},{17,9},{25,17},{2,26},{10... | collective-permute-start | bytes 196616 | tf_op jit(solution)/shard_map/ppermute | solution.py:473
  9.3 8.1 %collective-permute-start.3 = (f32[9,48,128]{2,1,0:T(8,128)S(1)}, f32[9,48,128]{2,1,0:T(8,128)S(1)}, u32[]{:S(2)}, u32[]{:S(2)}) collective-permute-start(f32[9,48,128]{2,1,0:T(8,128)S(1)} %shard_map.65), channel_id=1, source_target_pairs={{0,1},{1,0},{2,3},{3,2},{4,5},{5,4},{6,7},{7,6},{8,9},{9,8},{10,11... | collective-permute-start | bytes 663560 | tf_op jit(solution)/shard_map/ppermute | solution.py:470
  9.4 6.8 %collective-permute-start.2 = (f32[2,64,128]{2,1,0:T(8,128)S(1)}, f32[2,64,128]{2,1,0:T(8,128)S(1)}, u32[]{:S(2)}, u32[]{:S(2)}) collective-permute-start(f32[2,64,128]{2,1,0:T(8,128)S(1)} %get-tuple-element.19), channel_id=1, source_target_pairs={{0,16},{8,24},{16,0},{24,8},{1,17},{9,25},{17,1},{25,9},{2,18},{10... | collective-permute-start | bytes 196616 | tf_op jit(solution)/shard_map/ppermute | solution.py:473
  16.2 1.2 %collective-permute-start.4 = (f32[2,48,128]{2,1,0:T(8,128)S(1)}, f32[2,48,128]{2,1,0:T(8,128)S(1)}, u32[]{:S(2)}, u32[]{:S(2)}) collective-permute-start(f32[2,48,128]{2,1,0:T(8,128)S(1)} %shard_map.66), channel_id=1, source_target_pairs={{0,1},{1,0},{2,3},{3,2},{4,5},{5,4},{6,7},{7,6},{8,9},{9,8},{10,11... | collective-permute-start | bytes 147464 | tf_op jit(solution)/shard_map/ppermute | solution.py:470
  17.4 0.7 %collective-permute-start.5 = (f32[11,2,16,128]{3,2,1,0:T(8,128)S(1)}, f32[11,2,16,128]{3,2,1,0:T(8,128)S(1)}, u32[]{:S(2)}, u32[]{:S(2)}) collective-permute-start(f32[11,2,16,128]{3,2,1,0:T(8,128)S(1)} %shard_map.67), channel_id=1, source_target_pairs={{1,8},{9,16},{8,1},{17,24},{16,9},{25,26},{24,17},{27,18},{26,25},... | collective-permute-start | bytes 540680 | tf_op jit(solution)/shard_map/ppermute | solution.py:489
  20.7 11.0 %collective-permute-start.6 = (f32[2,32,128]{2,1,0:T(8,128)S(1)}, f32[2,32,128]{2,1,0:T(8,128)S(1)}, u32[]{:S(2)}, u32[]{:S(2)}) collective-permute-start(f32[2,32,128]{2,1,0:T(8,128)S(1)} %get-tuple-element.22), channel_id=1, source_target_pairs={{0,8},{8,16},{16,24},{24,0},{1,9},{9,17},{17,25},{25,1},{2,10},{10... | collective-permute-start | bytes 98312 | tf_op jit(solution)/shard_map/ppermute | solution.py:473
  26.9 4.9 %collective-permute-start.7 = (f32[2,32,128]{2,1,0:T(8,128)S(1)}, f32[2,32,128]{2,1,0:T(8,128)S(1)}, u32[]{:S(2)}, u32[]{:S(2)}) collective-permute-start(f32[2,32,128]{2,1,0:T(8,128)S(1)} %get-tuple-element.24), channel_id=1, source_target_pairs={{0,1},{1,0},{2,3},{3,2},{4,5},{5,4},{6,7},{7,6},{8,9},{9,8},{10,11... | collective-permute-start | bytes 98312 | tf_op jit(solution)/shard_map/ppermute | solution.py:470
  31.6 2.1 %collective-permute-start.10 = (f32[2,32,128]{2,1,0:T(8,128)S(1)}, f32[2,32,128]{2,1,0:T(8,128)S(1)}, u32[]{:S(2)}, u32[]{:S(2)}) collective-permute-start(f32[2,32,128]{2,1,0:T(8,128)S(1)} %shard_map.70), channel_id=1, source_target_pairs={{0,1},{1,0},{2,3},{3,2},{4,5},{5,4},{6,7},{7,6},{8,9},{9,8},{10,11... | collective-permute-start | bytes 98312 | tf_op jit(solution)/shard_map/ppermute | solution.py:470
  31.8 5.1 %collective-permute-start.8 = (f32[64,128]{1,0:T(8,128)S(1)}, f32[64,128]{1,0:T(8,128)S(1)}, u32[]{:S(2)}, u32[]{:S(2)}) collective-permute-start(f32[64,128]{1,0:T(8,128)S(1)} %get-tuple-element.25), channel_id=1, source_target_pairs={{0,16},{8,24},{16,0},{24,8},{1,17},{9,25},{17,1},{25,9},{2,18},{10... | collective-permute-start | bytes 98312 | tf_op jit(solution)/shard_map/ppermute | solution.py:473
  31.9 5.0 %collective-permute-start.9 = (f32[64,128]{1,0:T(8,128)S(1)}, f32[64,128]{1,0:T(8,128)S(1)}, u32[]{:S(2)}, u32[]{:S(2)}) collective-permute-start(f32[64,128]{1,0:T(8,128)S(1)} %get-tuple-element.26), channel_id=1, source_target_pairs={{0,24},{8,0},{16,8},{24,16},{1,25},{9,1},{17,9},{25,17},{2,26},{10... | collective-permute-start | bytes 98312 | tf_op jit(solution)/shard_map/ppermute | solution.py:473
